TPU v7x, 32 devices: a whole 2x2x4 slice. The times are simulated.
32 devices in a mesh: dp: 4 (over z), mp: 8 (over y, x, core).
Axes of the slice: x: 2, y: 2, z: 4, core: 2. Of those that a mesh axis runs over, the one named last changes fastest.
Arguments:
- weight: bfloat16 [5120, 32768], P('dp', 'mp'), may hold values from -0.078125 to 0.078125
- rank_map: int32 [8], replicated, may hold values from 0 to 7, each once
Outputs:
- quant_out: bfloat16 [5120, 32768], P(None, 'mp')
- scale_out: bfloat16 [5120, 256], P(None, 'mp')
- checksum: float32 [256], replicated
Inputs may be any that keep to these rules, and one draw needn't show every extreme that they name: `rank_map`: a permutation of 0 to 7.
All inputs are finite; a program needn't handle non-finite values.
Results may differ from a plain program's by a relative error of at most 0.0085.
Values may be sent and summed in bfloat16 or wider, within the bound.
A program may use at most 192 MiB of HBM per device.

v0:
```python
import functools
import math

import jax
import jax.numpy as jnp
from jax import lax
from jax.experimental import pallas as pl
from jax.experimental.pallas import tpu as pltpu
from jax.sharding import PartitionSpec as P


LANES = 128
FLOOR_RATIO = 0.25
MESH = pl.DeviceIdType.MESH
GRAIN = 32
VMEM_LIMIT = 57 * 1024 * 1024
FILL_LIMIT = 8 * 1024 * 1024


def flip(m, k):
    bit, out = 1, m
    while bit <= k:
        if k & bit:
            out = out + bit - 2 * bit * ((m // bit) % 2)
        bit *= 2
    return out


def scales_of(blocks, height, floor):
    lane = lax.broadcasted_iota(jnp.int32, (height, LANES), 1)
    peaks = jnp.zeros((height, LANES), jnp.float32)
    for b, read in enumerate(blocks):
        peak = jnp.max(jnp.abs(read().astype(jnp.float32)), axis=1, keepdims=True)
        peaks = jnp.where(lane == b, peak, peaks)
    return (jnp.maximum(peaks, floor) / 127.0).astype(jnp.bfloat16).astype(jnp.float32)


def quantize_rows(x_ref, rows, floor):
    nblocks = x_ref.shape[1] // LANES
    blocks = [lambda b=b: x_ref[rows, b * LANES:(b + 1) * LANES] for b in range(nblocks)]
    scale = scales_of(blocks, GRAIN, floor)
    inverse = 1.0 / scale
    yield scale
    for b, read in enumerate(blocks):
        yield (read().astype(jnp.float32) * inverse[:, b:b + 1]).astype(jnp.bfloat16)


def quantize_tile(floor, x_ref, q_ref, s_ref, scales):
    @pl.loop(0, LANES // GRAIN)
    def _(t):
        rows = pl.ds(pl.multiple_of(t * GRAIN, GRAIN), GRAIN)
        parts = quantize_rows(x_ref, rows, floor)
        scales[rows, :] = next(parts)
        for b, part in enumerate(parts):
            q_ref[rows, b * LANES:(b + 1) * LANES] = part

    s_ref[...] = scales[...].T[:s_ref.shape[0]].astype(jnp.bfloat16)


def quantize_all(landed, floor):
    rows, cols = landed.shape
    nblocks = cols // LANES
    return pl.pallas_call(
        functools.partial(quantize_tile, floor),
        grid=(rows // LANES,),
        in_specs=[pl.BlockSpec((LANES, cols), lambda t: (t, 0))],
        out_specs=[pl.BlockSpec((LANES, cols), lambda t: (t, 0)), pl.BlockSpec((nblocks, LANES), lambda t: (0, t))],
        out_shape=[jax.ShapeDtypeStruct((rows, cols), jnp.bfloat16), jax.ShapeDtypeStruct((nblocks, rows), jnp.bfloat16)],
        scratch_shapes=[pltpu.VMEM((LANES, LANES), jnp.float32)],
        compiler_params=pltpu.CompilerParams(dimension_semantics=("arbitrary",)),
        cost_estimate=pl.CostEstimate(flops=rows * cols * 4, bytes_accessed=rows * cols * 4, transcendentals=0),
    )(landed)


def fill_kernel(n, rows, first, floor, got_ref, _q, _s, q_ref, s_ref, q_v, s_v, scales, sems):
    z = lax.axis_index("dp")

    @pl.when(jnp.logical_or(z == 0, z == n - 1))
    def _():
        quantize_tile(floor, got_ref, q_v, s_v, scales)
        place = pl.ds(pl.multiple_of(jnp.where(z == 0, 1, n - 2) * rows + first, LANES), LANES)
        copies = [pltpu.make_async_copy(q_v, q_ref.at[place], sems.at[0]),
                  pltpu.make_async_copy(s_v, s_ref.at[:, place], sems.at[1])]
        for copy in copies:
            copy.start()
        for copy in copies:
            copy.wait()


def fill(quant, scale, got, n, rows, first, floor):
    size, cols = got.shape
    any_spec = pl.BlockSpec(memory_space=pl.ANY)
    return pl.pallas_call(
        functools.partial(fill_kernel, n, rows, first, floor),
        in_specs=[pl.BlockSpec(memory_space=pltpu.VMEM), any_spec, any_spec],
        out_specs=[any_spec] * 2,
        out_shape=[jax.ShapeDtypeStruct(quant.shape, quant.dtype), jax.ShapeDtypeStruct(scale.shape, scale.dtype)],
        input_output_aliases={1: 0, 2: 1},
        scratch_shapes=[
            pltpu.VMEM((size, cols), quant.dtype),
            pltpu.VMEM((scale.shape[0], LANES), scale.dtype),
            pltpu.VMEM((LANES, LANES), jnp.float32),
            pltpu.SemaphoreType.DMA((2,)),
        ],
        compiler_params=pltpu.CompilerParams(vmem_limit_bytes=FILL_LIMIT),
        cost_estimate=pl.CostEstimate(flops=size * cols * 4, bytes_accessed=size * cols * 4, transcendentals=0),
    )(got, quant, scale)


def move_kernel(n, count, spans, floor, map_ref, w_ref, out_ref, tail_ref, last_ref, sum_ref,
                stage, perm, acc, zsum, total, psum,
                load_sem, own_sem, tail_sem, a_send, a_recv, z_send, z_recv):
    z = lax.axis_index("dp")
    m = lax.axis_index("mp")
    rows, width = perm.shape[1:]
    group = width // LANES
    nblocks = count * group
    chunks = len(spans)
    TAIL, SUM = chunks - 1, chunks
    order = sorted(range(1, count), key=lambda k: (bin(k).count("1"), k))

    def when(cond, act):
        @pl.when(cond)
        def _():
            act()

    loads = [pltpu.make_async_copy(w_ref.at[pl.ds(*span)], stage.at[pl.ds(*span)], load_sem.at[c])
             for c, span in enumerate(spans)]
    for load in loads:
        load.start()

    barrier = pltpu.get_barrier_semaphore()
    for k in range(1, count):
        pl.semaphore_signal(barrier, inc=1, device_id=(z, flip(m, k)), device_id_type=MESH)
    when(z > 0, lambda: pl.semaphore_signal(barrier, inc=1, device_id=(z - 1, m), device_id_type=MESH))
    when(z < n - 1, lambda: pl.semaphore_signal(barrier, inc=1, device_id=(z + 1, m), device_id_type=MESH))
    beside = jnp.where(z > 0, 1, 0) + jnp.where(z < n - 1, 1, 0)

    holds = [[map_ref[j] == r for j in range(count)] for r in range(count)]

    def arrange(c):
        start, size = spans[c]
        loads[c].wait()

        @pl.loop(0, size // GRAIN)
        def _(t):
            here = pl.ds(pl.multiple_of(start + t * GRAIN, GRAIN), GRAIN)
            for i in range(group):
                first = i * count
                blocks = [stage[here, (first + j) * LANES:(first + j + 1) * LANES] for j in range(count)]
                for r in range(count):
                    block = blocks[0]
                    for j in range(1, count):
                        block = jnp.where(holds[r][j], blocks[j], block)
                    perm[r, here, i * LANES:(i + 1) * LANES] = block

    def place(origin, c, src):
        start, size = spans[c]
        return out_ref.at[pl.ds(pl.multiple_of(origin * rows + start, 16), size),
                          pl.ds(pl.multiple_of(src * width, LANES), width)]

    def own(c):
        return perm.at[m, pl.ds(*spans[c])]

    def plane(c, k):
        peer = flip(m, k)
        if c == SUM:
            src, dst = total, psum.at[m]
        else:
            src, dst = perm.at[peer, pl.ds(*spans[c])], place(z, c, m)
        return pltpu.make_async_remote_copy(
            src_ref=src, dst_ref=dst, send_sem=a_send.at[c, k - 1], recv_sem=a_recv.at[c, k - 1],
            device_id=(z, peer), device_id_type=MESH)

    def ring(unit, way, hop):
        c, k = unit
        origin = z - way * (hop - 1)
        if c == SUM:
            src = dst = zsum.at[origin]
        else:
            dst = place(origin, c, flip(m, k))
            src = own(c) if hop == 1 and k == 0 else dst
        w = 0 if way == 1 else 1
        return pltpu.make_async_remote_copy(
            src_ref=src, dst_ref=dst, send_sem=z_send.at[w, hop - 1, c, k], recv_sem=z_recv.at[w, hop - 1, c, k],
            device_id=(z + way, m), device_id_type=MESH)

    def sends(unit, way, hop):
        later = hop == 1 and unit[0] == TAIL
        if way == -1:
            return jnp.logical_and(z > (1 if later else 0), z + hop - 1 <= n - 1)
        return jnp.logical_and(z < n - (2 if later else 1), z - (hop - 1) >= 0)

    def gets(unit, way, hop):
        later = hop == 1 and unit[0] == TAIL
        if way == -1:
            return jnp.logical_and(z >= (1 if later else 0), z + hop <= n - 1)
        return jnp.logical_and(z <= n - (2 if later else 1), z - hop >= 0)

    def start_ring(unit):
        for way in (-1, 1):
            when(sends(unit, way, 1), lambda way=way: ring(unit, way, 1).start())

    def keep(c):
        return pltpu.make_async_copy(own(c), place(z, c, m), own_sem.at[c])

    def send_own(c):
        start_ring((c, 0))
        for k in order:
            plane(c, k).start()
        keep(c).start()

    def add_up(first, size):
        @pl.loop(0, size // GRAIN)
        def _(t):
            parts = quantize_rows(stage, pl.ds(pl.multiple_of(first + t * GRAIN, GRAIN), GRAIN), floor)
            next(parts)
            for b, part in enumerate(parts):
                acc[b] += jnp.sum(part.astype(jnp.float32).reshape(GRAIN // 8, 8, LANES), axis=0)

    acc[...] = jnp.zeros_like(acc)
    arrange(0)
    pl.semaphore_wait(barrier, count - 1 + beside)
    send_own(0)
    arrange(1)
    for c in range(2, chunks):
        arrange(c)
        send_own(c - 1)
    add_up(*spans[0])
    send_own(TAIL)
    add_up(spans[0][1], rows - spans[0][1])

    sums = jnp.sum(jnp.sum(acc[...], axis=1), axis=1, keepdims=True)
    row = lax.broadcasted_iota(jnp.int32, (nblocks, LANES), 0)
    col = lax.broadcasted_iota(jnp.int32, (nblocks, LANES), 1)
    line = jnp.sum(jnp.where(row == col, sums, 0.0), axis=0, keepdims=True)
    zsum[z] = jnp.broadcast_to(line, zsum.shape[1:])

    blocks = [(c, k) for c in range(chunks) for k in [0] + order]
    for c, k in blocks:
        if k > 0:
            plane(c, k).wait_recv()
            start_ring((c, k))
            if (c, k) == (0, order[-1]):
                start_ring((SUM, 0))

    keep(TAIL).wait()
    start = spans[TAIL][0]
    tail_out = []
    for i, ref in enumerate((tail_ref, last_ref)):
        here = pl.ds(pl.multiple_of(z * rows + start + i * LANES, 16), LANES)
        tail_out.append(pltpu.make_async_copy(out_ref.at[here], ref, tail_sem.at[i]))
    for copy in tail_out:
        copy.start()

    units = [(SUM, 0)] + blocks
    for hop in range(2, n):
        for unit in units:
            for way in (-1, 1):
                def forward(unit=unit, way=way, hop=hop):
                    ring(unit, way, hop - 1).wait_recv()
                    ring(unit, way, hop).start()

                when(sends(unit, way, hop), forward)

    def settle(unit, way, hop):
        stays = z == 0 if way == -1 else z == n - 1
        when(jnp.logical_and(gets(unit, way, hop), stays), lambda: ring(unit, way, hop).wait_recv())

    for hop in range(1, n):
        for way in (-1, 1):
            settle((SUM, 0), way, hop)
    whole = zsum[0]
    for origin in range(1, n):
        whole = whole + zsum[origin]
    total[...] = whole
    psum[m] = whole
    for copy in tail_out:
        copy.wait()
    for c in range(chunks):
        if c != TAIL:
            keep(c).wait()
        for k in order:
            plane(c, k).wait_send()
    for k in order:
        plane(SUM, k).start()
    for k in order:
        plane(SUM, k).wait()
    sum_ref[...] = psum[...]

    for hop in range(1, n):
        for unit in units:
            for way in (-1, 1):
                if unit[0] != SUM:
                    settle(unit, way, hop)
                when(sends(unit, way, hop),
                     lambda unit=unit, way=way, hop=hop: ring(unit, way, hop).wait_send())


def move(weight, rank_map, n, spans, floor):
    rows, cols = weight.shape
    count = rank_map.shape[0]
    width = cols // count
    nblocks = cols // LANES
    chunks = len(spans)
    any_spec = pl.BlockSpec(memory_space=pl.ANY)
    dma = pltpu.SemaphoreType.DMA
    sent = rows * cols * 2 * (n - 1)
    return pl.pallas_call(
        functools.partial(move_kernel, n, count, spans, floor),
        in_specs=[pl.BlockSpec(memory_space=pltpu.SMEM), any_spec],
        out_specs=[any_spec] + [pl.BlockSpec(memory_space=pltpu.VMEM)] * 3,
        out_shape=[
            jax.ShapeDtypeStruct((n * rows, cols), weight.dtype),
            jax.ShapeDtypeStruct((LANES, cols), weight.dtype),
            jax.ShapeDtypeStruct((LANES, cols), weight.dtype),
            jax.ShapeDtypeStruct((count, 8, LANES), jnp.float32),
        ],
        scratch_shapes=[
            pltpu.VMEM((rows, cols), weight.dtype),
            pltpu.VMEM((count, rows, width), weight.dtype),
            pltpu.VMEM((nblocks, 8, LANES), jnp.float32),
            pltpu.VMEM((n, 8, LANES), jnp.float32),
            pltpu.VMEM((8, LANES), jnp.float32),
            pltpu.VMEM((count, 8, LANES), jnp.float32),
            dma((chunks,)),
            dma((chunks,)),
            dma((2,)),
            dma((chunks + 1, count - 1)),
            dma((chunks + 1, count - 1)),
            dma((2, n - 1, chunks + 1, count)),
            dma((2, n - 1, chunks + 1, count)),
        ],
        compiler_params=pltpu.CompilerParams(collective_id=0, has_side_effects=True, vmem_limit_bytes=VMEM_LIMIT),
        cost_estimate=pl.CostEstimate(flops=rows * cols * 8, bytes_accessed=sent * 2, transcendentals=0),
    )(rank_map, weight)


def local(n, weight, rank_map):
    rows, cols = weight.shape
    nblocks = cols // LANES
    total_rows = rows * n
    floor = FLOOR_RATIO / math.sqrt(total_rows)
    main = rows - 2 * LANES
    rest = (main - LANES) // 2
    spans = ((0, LANES), (LANES, rest), (LANES + rest, rest), (main, 2 * LANES))
    ends = [(1, 0), (n - 2, n - 1)]

    landed, tail_own, last_own, sums = move(weight, rank_map, n, spans, floor)
    tail_got = lax.ppermute(tail_own, "dp", ends)
    last_got = lax.ppermute(last_own, "dp", ends)
    quant, scale = quantize_all(landed, floor)
    quant, scale = fill(quant, scale, tail_got, n, rows, main, floor)
    quant, scale = fill(quant, scale, last_got, n, rows, main + LANES, floor)
    totals = sums[:, 0, :nblocks].reshape(-1)
    return (quant, scale.T, totals / (127.0 * math.sqrt(total_rows * LANES)))


def solution(mesh):
    n = mesh.shape["dp"]
    in_specs = (P("dp", "mp"), P())
    out_specs = (P(None, "mp"), P(None, "mp"), P())

    def body(weight, rank_map):
        return local(n, weight, rank_map)

    return jax.shard_map(body, mesh=mesh, in_specs=in_specs, out_specs=out_specs, check_vma=False)
```

profile of v0, /device:TPU:0, one launch (start us, length us, event | category | flops | bytes accessed | tf_op | source)
XLA Modules:
  0.0 743.0 jit_solution(7138273089188608469)
XLA Ops:
  0.6 647.5 %shard_map.49 = (bf16[5120,4096]{1,0:T(8,128)(2,1)}, bf16[128,4096]{1,0:T(8,128)(2,1)}, bf16[128,4096]{1,0:T(8,128)(2,1)}, f32[8,8,128]{2,1,0:T(8,128)}) custom-call(s32[8]{0:T(128)} %map_ref.1, bf16[1280,4096]{1,0:T(8,128)(2,1)} %w_ref.1), custom_call_target="tpu_custom_call" | custom-call | flops 41943040 | bytes 62914560 | tf_op jit(solution)/shard_map/pallas_call | solution.py:309
  648.2 1.3 collective-permute-start.1
  649.5 1.3 collective-permute-start
  650.8 0.8 multiply_reduce_fusion
  651.6 0.6 div.10
  652.2 84.7 %shard_map.50 = (bf16[5120,4096]{1,0:T(8,128)(2,1)}, bf16[32,5120]{1,0:T(8,128)(2,1)}) custom-call(bf16[5120,4096]{1,0:T(8,128)(2,1)} %get-tuple-element.15.x_ref), custom_call_target="tpu_custom_call" | custom-call | flops 83886080 | bytes 83886080 | tf_op jit(solution)/shard_map/pallas_call | solution.py:63
  736.9 0.0 collective-permute-done.1.got_ref
  736.9 3.0 shard_map.51
  739.9 0.0 collective-permute-done.got_ref
  739.9 3.0 shard_map.52
Async XLA Ops:
  648.2 88.7 %collective-permute-start.1 = (bf16[128,4096]{1,0:T(8,128)(2,1)}, bf16[128,4096]{1,0:T(8,128)(2,1)S(1)}, u32[]{:S(2)}, u32[]{:S(2)}) collective-permute-start(bf16[128,4096]{1,0:T(8,128)(2,1)} %get-tuple-element.14), channel_id=1, source_target_pairs={{8,0},{16,24},{9,1},{17,25},{10,2},{18,26},{11,3},{19,27},{12,4},{... | collective-permute-start | bytes 3145736 | tf_op jit(solution)/shard_map/ppermute | solution.py:350
  649.5 90.4 %collective-permute-start = (bf16[128,4096]{1,0:T(8,128)(2,1)}, bf16[128,4096]{1,0:T(8,128)(2,1)S(1)}, u32[]{:S(2)}, u32[]{:S(2)}) collective-permute-start(bf16[128,4096]{1,0:T(8,128)(2,1)} %get-tuple-element.13), channel_id=1, source_target_pairs={{8,0},{16,24},{9,1},{17,25},{10,2},{18,26},{11,3},{19,27},{12,4},{... | collective-permute-start | bytes 3145736 | tf_op jit(solution)/shard_map/ppermute | solution.py:351
where the time goes:
time: 743 us
  Pallas kernels  738 us (99%)
    pallas_call x1, Pallas kernels, move(): pl.pallas_call(functools.partial(move_kernel, n, count, spans, floor), in...  648 us
    pallas_call x1, Pallas kernels, quantize_all(): pl.pallas_call(functools.partial(quantize_tile, floor), grid=(rows // LAN...  84.7 us
  transfers between devices with their start and end apart: 2, of which 0 were waited for; matrix products, arithmetic and copies ran while one was open for 0% of the time, Pallas kernels for 12%

commit v1 on v0

--- a/solution.py
+++ b/solution.py
@@ -13,6 +13,7 @@
 FLOOR_RATIO = 0.25
 MESH = pl.DeviceIdType.MESH
 GRAIN = 32
+TILE = 2 * LANES
 VMEM_LIMIT = 57 * 1024 * 1024
 FILL_LIMIT = 8 * 1024 * 1024
 
@@ -26,59 +27,78 @@
     return out
 
 
-def scales_of(blocks, height, floor):
-    lane = lax.broadcasted_iota(jnp.int32, (height, LANES), 1)
-    peaks = jnp.zeros((height, LANES), jnp.float32)
-    for b, read in enumerate(blocks):
-        peak = jnp.max(jnp.abs(read().astype(jnp.float32)), axis=1, keepdims=True)
-        peaks = jnp.where(lane == b, peak, peaks)
-    return (jnp.maximum(peaks, floor) / 127.0).astype(jnp.bfloat16).astype(jnp.float32)
-
-
-def quantize_rows(x_ref, rows, floor):
+def write_spread(spread, nblocks):
+    lane = lax.broadcasted_iota(jnp.int32, (LANES, LANES), 0)
+    for b in range(nblocks):
+        hit = jnp.logical_and(lax.rem(lane, nblocks) == b, lane < 3 * nblocks)
+        spread[:, b * LANES:(b + 1) * LANES] = jnp.where(hit, 1.0, 0.0).astype(jnp.bfloat16)
+
+
+def quantize_rows(x_ref, rows, spread, floor):
     nblocks = x_ref.shape[1] // LANES
-    blocks = [lambda b=b: x_ref[rows, b * LANES:(b + 1) * LANES] for b in range(nblocks)]
-    scale = scales_of(blocks, GRAIN, floor)
+    shape = (LANES, LANES)
+    lane = lax.broadcasted_iota(jnp.int32, shape, 1)
+    slot = lax.rem(lane, nblocks)
+    peaks = jnp.zeros(shape, jnp.bfloat16)
+    for b in range(nblocks):
+        peak = jnp.max(jnp.abs(x_ref[rows, b * LANES:(b + 1) * LANES]), axis=1, keepdims=True)
+        peaks = jnp.where(slot == b, peak, peaks)
+    scale = (jnp.maximum(peaks.astype(jnp.float32), floor) / 127.0).astype(jnp.bfloat16).astype(jnp.float32)
+    yield scale
     inverse = 1.0 / scale
-    yield scale
-    for b, read in enumerate(blocks):
-        yield (read().astype(jnp.float32) * inverse[:, b:b + 1]).astype(jnp.bfloat16)
-
-
-def quantize_tile(floor, x_ref, q_ref, s_ref, scales):
-    @pl.loop(0, LANES // GRAIN)
+    high = inverse.astype(jnp.bfloat16).astype(jnp.float32)
+    middle = (inverse - high).astype(jnp.bfloat16).astype(jnp.float32)
+    low = inverse - high - middle
+    parts = jnp.where(lane < nblocks, high, jnp.where(lane < 2 * nblocks, middle, low)).astype(jnp.bfloat16)
+    for b in range(0, nblocks, 2):
+        factor = jnp.dot(parts, spread[:, b * LANES:(b + 2) * LANES], preferred_element_type=jnp.float32)
+        pair = x_ref[rows, b * LANES:(b + 2) * LANES].astype(jnp.float32) * factor
+        for i in range(2):
+            yield pair[:, i * LANES:(i + 1) * LANES].astype(jnp.bfloat16)
+
+
+def quantize_tile(floor, x_ref, q_ref, s_ref, spread):
+    @pl.loop(0, x_ref.shape[0] // LANES)
     def _(t):
-        rows = pl.ds(pl.multiple_of(t * GRAIN, GRAIN), GRAIN)
-        parts = quantize_rows(x_ref, rows, floor)
-        scales[rows, :] = next(parts)
+        rows = pl.ds(pl.multiple_of(t * LANES, LANES), LANES)
+        parts = quantize_rows(x_ref, rows, spread, floor)
+        s_ref[:, rows] = next(parts).T[:s_ref.shape[0]].astype(jnp.bfloat16)
         for b, part in enumerate(parts):
             q_ref[rows, b * LANES:(b + 1) * LANES] = part
 
-    s_ref[...] = scales[...].T[:s_ref.shape[0]].astype(jnp.bfloat16)
+
+def quantize_kernel(floor, x_ref, q_ref, s_ref, spread):
+    @pl.when(pl.program_id(0) == 0)
+    def _():
+        write_spread(spread, s_ref.shape[0])
+
+    quantize_tile(floor, x_ref, q_ref, s_ref, spread)
 
 
 def quantize_all(landed, floor):
     rows, cols = landed.shape
     nblocks = cols // LANES
+    tile = TILE
     return pl.pallas_call(
-        functools.partial(quantize_tile, floor),
-        grid=(rows // LANES,),
-        in_specs=[pl.BlockSpec((LANES, cols), lambda t: (t, 0))],
-        out_specs=[pl.BlockSpec((LANES, cols), lambda t: (t, 0)), pl.BlockSpec((nblocks, LANES), lambda t: (0, t))],
+        functools.partial(quantize_kernel, floor),
+        grid=(rows // tile,),
+        in_specs=[pl.BlockSpec((tile, cols), lambda t: (t, 0))],
+        out_specs=[pl.BlockSpec((tile, cols), lambda t: (t, 0)), pl.BlockSpec((nblocks, tile), lambda t: (0, t))],
         out_shape=[jax.ShapeDtypeStruct((rows, cols), jnp.bfloat16), jax.ShapeDtypeStruct((nblocks, rows), jnp.bfloat16)],
-        scratch_shapes=[pltpu.VMEM((LANES, LANES), jnp.float32)],
+        scratch_shapes=[pltpu.VMEM((LANES, cols), jnp.bfloat16)],
         compiler_params=pltpu.CompilerParams(dimension_semantics=("arbitrary",)),
         cost_estimate=pl.CostEstimate(flops=rows * cols * 4, bytes_accessed=rows * cols * 4, transcendentals=0),
     )(landed)
 
 
-def fill_kernel(n, rows, first, floor, got_ref, _q, _s, q_ref, s_ref, q_v, s_v, scales, sems):
+def fill_kernel(n, rows, first, floor, got_ref, _q, _s, q_ref, s_ref, q_v, s_v, spread, sems):
     z = lax.axis_index("dp")
 
     @pl.when(jnp.logical_or(z == 0, z == n - 1))
     def _():
-        quantize_tile(floor, got_ref, q_v, s_v, scales)
-        place = pl.ds(pl.multiple_of(jnp.where(z == 0, 1, n - 2) * rows + first, LANES), LANES)
+        write_spread(spread, s_v.shape[0])
+        quantize_tile(floor, got_ref, q_v, s_v, spread)
+        place = pl.ds(pl.multiple_of(jnp.where(z == 0, 1, n - 2) * rows + first, LANES), q_v.shape[0])
         copies = [pltpu.make_async_copy(q_v, q_ref.at[place], sems.at[0]),
                   pltpu.make_async_copy(s_v, s_ref.at[:, place], sems.at[1])]
         for copy in copies:
@@ -98,8 +118,8 @@
         input_output_aliases={1: 0, 2: 1},
         scratch_shapes=[
             pltpu.VMEM((size, cols), quant.dtype),
-            pltpu.VMEM((scale.shape[0], LANES), scale.dtype),
-            pltpu.VMEM((LANES, LANES), jnp.float32),
+            pltpu.VMEM((scale.shape[0], size), scale.dtype),
+            pltpu.VMEM((LANES, cols), jnp.bfloat16),
             pltpu.SemaphoreType.DMA((2,)),
         ],
         compiler_params=pltpu.CompilerParams(vmem_limit_bytes=FILL_LIMIT),
@@ -108,7 +128,7 @@
 
 
 def move_kernel(n, count, spans, floor, map_ref, w_ref, out_ref, tail_ref, last_ref, sum_ref,
-                stage, perm, acc, zsum, total, psum,
+                stage, perm, spread, acc, zsum, total, psum,
                 load_sem, own_sem, tail_sem, a_send, a_recv, z_send, z_recv):
     z = lax.axis_index("dp")
     m = lax.axis_index("mp")
@@ -211,14 +231,13 @@
         keep(c).start()
 
     def add_up(first, size):
-        @pl.loop(0, size // GRAIN)
+        @pl.loop(0, size // LANES)
         def _(t):
-            parts = quantize_rows(stage, pl.ds(pl.multiple_of(first + t * GRAIN, GRAIN), GRAIN), floor)
+            parts = quantize_rows(stage, pl.ds(pl.multiple_of(first + t * LANES, LANES), LANES), spread, floor)
             next(parts)
             for b, part in enumerate(parts):
-                acc[b] += jnp.sum(part.astype(jnp.float32).reshape(GRAIN // 8, 8, LANES), axis=0)
-
-    acc[...] = jnp.zeros_like(acc)
+                acc[b] += jnp.sum(part.astype(jnp.float32).reshape(LANES // 8, 8, LANES), axis=0)
+
     arrange(0)
     pl.semaphore_wait(barrier, count - 1 + beside)
     send_own(0)
@@ -226,6 +245,8 @@
     for c in range(2, chunks):
         arrange(c)
         send_own(c - 1)
+    acc[...] = jnp.zeros_like(acc)
+    write_spread(spread, nblocks)
     add_up(*spans[0])
     send_own(TAIL)
     add_up(spans[0][1], rows - spans[0][1])
@@ -319,6 +340,7 @@
         scratch_shapes=[
             pltpu.VMEM((rows, cols), weight.dtype),
             pltpu.VMEM((count, rows, width), weight.dtype),
+            pltpu.VMEM((LANES, cols), jnp.bfloat16),
             pltpu.VMEM((nblocks, 8, LANES), jnp.float32),
             pltpu.VMEM((n, 8, LANES), jnp.float32),
             pltpu.VMEM((8, LANES), jnp.float32),

time: 743 us -> 702 us (0.945)
  Pallas kernels: 738 us -> 696 us
    pallas_call x1, Pallas kernels: 84.7 us -> 47.4 us  [quantize_all(): pl.pallas_call(functools.partial(quantize_kernel, floor), grid=(rows // t...]
  transfers between devices with their start and end apart: 2 -> 2, of which waited for: 0 -> 0; matrix products, arithmetic and copies ran while one was open for 0% -> 0% of each run, Pallas kernels for 12% -> 7%
where the time goes in v1:
time: 702 us; the launch traced here: 701 us
  Pallas kernels  696 us (99%)
    pallas_call x1, Pallas kernels, move(): pl.pallas_call(functools.partial(move_kernel, n, count, spans, floor), in...  644 us
    pallas_call x1, Pallas kernels, quantize_all(): pl.pallas_call(functools.partial(quantize_kernel, floor), grid=(rows // t...  47.4 us
  transfers between devices with their start and end apart: 2, of which 0 were waited for; matrix products, arithmetic and copies ran while one was open for 0% of the time, Pallas kernels for 7%

profile of v1, /device:TPU:0, one launch (start us, length us, event | category | flops | bytes accessed | tf_op | source)
XLA Modules:
  0.0 700.7 jit_solution(12713487530433783401)
XLA Ops:
  0.6 644.4 %shard_map.49 = (bf16[5120,4096]{1,0:T(8,128)(2,1)}, bf16[128,4096]{1,0:T(8,128)(2,1)}, bf16[128,4096]{1,0:T(8,128)(2,1)}, f32[8,8,128]{2,1,0:T(8,128)}) custom-call(s32[8]{0:T(128)} %map_ref.1, bf16[1280,4096]{1,0:T(8,128)(2,1)} %w_ref.1), custom_call_target="tpu_custom_call" | custom-call | flops 41943040 | bytes 62914560 | tf_op jit(solution)/shard_map/pallas_call | solution.py:330
  645.1 1.3 collective-permute-start.1
  646.4 1.3 collective-permute-start
  647.7 0.8 multiply_reduce_fusion
  648.5 0.6 div.10
  649.1 47.4 %shard_map.50 = (bf16[5120,4096]{1,0:T(8,128)(2,1)}, bf16[32,5120]{1,0:T(8,128)(2,1)}) custom-call(bf16[5120,4096]{1,0:T(8,128)(2,1)} %get-tuple-element.15.x_ref), custom_call_target="tpu_custom_call" | custom-call | flops 83886080 | bytes 83886080 | tf_op jit(solution)/shard_map/pallas_call | solution.py:82
  696.5 0.0 collective-permute-done.1.got_ref
  696.5 2.1 shard_map.51
  698.6 0.0 collective-permute-done.got_ref
  698.6 2.1 shard_map.52
Async XLA Ops:
  645.1 51.4 %collective-permute-start.1 = (bf16[128,4096]{1,0:T(8,128)(2,1)}, bf16[128,4096]{1,0:T(8,128)(2,1)S(1)}, u32[]{:S(2)}, u32[]{:S(2)}) collective-permute-start(bf16[128,4096]{1,0:T(8,128)(2,1)} %get-tuple-element.14), channel_id=1, source_target_pairs={{8,0},{16,24},{9,1},{17,25},{10,2},{18,26},{11,3},{19,27},{12,4},{... | collective-permute-start | bytes 3145736 | tf_op jit(solution)/shard_map/ppermute | solution.py:372
  646.4 52.2 %collective-permute-start = (bf16[128,4096]{1,0:T(8,128)(2,1)}, bf16[128,4096]{1,0:T(8,128)(2,1)S(1)}, u32[]{:S(2)}, u32[]{:S(2)}) collective-permute-start(bf16[128,4096]{1,0:T(8,128)(2,1)} %get-tuple-element.13), channel_id=1, source_target_pairs={{8,0},{16,24},{9,1},{17,25},{10,2},{18,26},{11,3},{19,27},{12,4},{... | collective-permute-start | bytes 3145736 | tf_op jit(solution)/shard_map/ppermute | solution.py:373

commit v2 on v1

--- a/solution.py
+++ b/solution.py
@@ -13,8 +13,9 @@
 FLOOR_RATIO = 0.25
 MESH = pl.DeviceIdType.MESH
 GRAIN = 32
-TILE = 2 * LANES
+TILE = 4 * LANES
 VMEM_LIMIT = 57 * 1024 * 1024
+QUANT_LIMIT = 40 * 1024 * 1024
 FILL_LIMIT = 8 * 1024 * 1024
 
 
@@ -39,11 +40,11 @@
     shape = (LANES, LANES)
     lane = lax.broadcasted_iota(jnp.int32, shape, 1)
     slot = lax.rem(lane, nblocks)
-    peaks = jnp.zeros(shape, jnp.bfloat16)
+    peaks = jnp.zeros(shape, jnp.float32)
     for b in range(nblocks):
         peak = jnp.max(jnp.abs(x_ref[rows, b * LANES:(b + 1) * LANES]), axis=1, keepdims=True)
-        peaks = jnp.where(slot == b, peak, peaks)
-    scale = (jnp.maximum(peaks.astype(jnp.float32), floor) / 127.0).astype(jnp.bfloat16).astype(jnp.float32)
+        peaks = jnp.where(slot == b, peak.astype(jnp.float32), peaks)
+    scale = (jnp.maximum(peaks, floor) / 127.0).astype(jnp.bfloat16).astype(jnp.float32)
     yield scale
     inverse = 1.0 / scale
     high = inverse.astype(jnp.bfloat16).astype(jnp.float32)
@@ -53,18 +54,19 @@
     for b in range(0, nblocks, 2):
         factor = jnp.dot(parts, spread[:, b * LANES:(b + 2) * LANES], preferred_element_type=jnp.float32)
         pair = x_ref[rows, b * LANES:(b + 2) * LANES].astype(jnp.float32) * factor
-        for i in range(2):
-            yield pair[:, i * LANES:(i + 1) * LANES].astype(jnp.bfloat16)
+        yield pair.astype(jnp.bfloat16)
 
 
 def quantize_tile(floor, x_ref, q_ref, s_ref, spread):
-    @pl.loop(0, x_ref.shape[0] // LANES)
+    tiles = x_ref.shape[0] // LANES
+
+    @pl.loop(0, tiles, unroll=tiles)
     def _(t):
         rows = pl.ds(pl.multiple_of(t * LANES, LANES), LANES)
         parts = quantize_rows(x_ref, rows, spread, floor)
         s_ref[:, rows] = next(parts).T[:s_ref.shape[0]].astype(jnp.bfloat16)
         for b, part in enumerate(parts):
-            q_ref[rows, b * LANES:(b + 1) * LANES] = part
+            q_ref[rows, b * 2 * LANES:(b + 1) * 2 * LANES] = part
 
 
 def quantize_kernel(floor, x_ref, q_ref, s_ref, spread):
@@ -86,15 +88,19 @@
         out_specs=[pl.BlockSpec((tile, cols), lambda t: (t, 0)), pl.BlockSpec((nblocks, tile), lambda t: (0, t))],
         out_shape=[jax.ShapeDtypeStruct((rows, cols), jnp.bfloat16), jax.ShapeDtypeStruct((nblocks, rows), jnp.bfloat16)],
         scratch_shapes=[pltpu.VMEM((LANES, cols), jnp.bfloat16)],
-        compiler_params=pltpu.CompilerParams(dimension_semantics=("arbitrary",)),
+        compiler_params=pltpu.CompilerParams(dimension_semantics=("arbitrary",), vmem_limit_bytes=QUANT_LIMIT),
         cost_estimate=pl.CostEstimate(flops=rows * cols * 4, bytes_accessed=rows * cols * 4, transcendentals=0),
     )(landed)
 
 
-def fill_kernel(n, rows, first, floor, got_ref, _q, _s, q_ref, s_ref, q_v, s_v, spread, sems):
+def fill_kernel(n, rows, first, even, floor, got_ref, _q, _s, q_ref, s_ref, q_v, s_v, spread, sems):
     z = lax.axis_index("dp")
 
-    @pl.when(jnp.logical_or(z == 0, z == n - 1))
+    end = jnp.logical_or(z == 0, z == n - 1)
+    if even:
+        end = jnp.logical_and(end, lax.axis_index("mp") % 2 == 0)
+
+    @pl.when(end)
     def _():
         write_spread(spread, s_v.shape[0])
         quantize_tile(floor, got_ref, q_v, s_v, spread)
@@ -107,11 +113,11 @@
             copy.wait()
 
 
-def fill(quant, scale, got, n, rows, first, floor):
+def fill(quant, scale, got, n, rows, first, even, floor):
     size, cols = got.shape
     any_spec = pl.BlockSpec(memory_space=pl.ANY)
     return pl.pallas_call(
-        functools.partial(fill_kernel, n, rows, first, floor),
+        functools.partial(fill_kernel, n, rows, first, even, floor),
         in_specs=[pl.BlockSpec(memory_space=pltpu.VMEM), any_spec, any_spec],
         out_specs=[any_spec] * 2,
         out_shape=[jax.ShapeDtypeStruct(quant.shape, quant.dtype), jax.ShapeDtypeStruct(scale.shape, scale.dtype)],
@@ -127,7 +133,7 @@
     )(got, quant, scale)
 
 
-def move_kernel(n, count, spans, floor, map_ref, w_ref, out_ref, tail_ref, last_ref, sum_ref,
+def move_kernel(n, count, spans, floor, map_ref, w_ref, out_ref, odd_ref, tail_ref, last_ref, sum_ref,
                 stage, perm, spread, acc, zsum, total, psum,
                 load_sem, own_sem, tail_sem, a_send, a_recv, z_send, z_recv):
     z = lax.axis_index("dp")
@@ -135,8 +141,7 @@
     rows, width = perm.shape[1:]
     group = width // LANES
     nblocks = count * group
-    chunks = len(spans)
-    TAIL, SUM = chunks - 1, chunks
+    MAIN, ODD, TAIL, HEAD, BODY, SUM = range(6)
     order = sorted(range(1, count), key=lambda k: (bin(k).count("1"), k))
 
     def when(cond, act):
@@ -144,9 +149,9 @@
         def _():
             act()
 
-    loads = [pltpu.make_async_copy(w_ref.at[pl.ds(*span)], stage.at[pl.ds(*span)], load_sem.at[c])
-             for c, span in enumerate(spans)]
-    for load in loads:
+    loads = {c: pltpu.make_async_copy(w_ref.at[pl.ds(*spans[c])], stage.at[pl.ds(*spans[c])], load_sem.at[c])
+             for c in (HEAD, BODY, ODD, TAIL)}
+    for load in loads.values():
         load.start()
 
     barrier = pltpu.get_barrier_semaphore()
@@ -205,17 +210,20 @@
             src_ref=src, dst_ref=dst, send_sem=z_send.at[w, hop - 1, c, k], recv_sem=z_recv.at[w, hop - 1, c, k],
             device_id=(z + way, m), device_id_type=MESH)
 
+    def kept(unit, hop):
+        return {TAIL: 1, ODD: 1 - m % 2}.get(unit[0], 0) if hop == 1 else 0
+
     def sends(unit, way, hop):
-        later = hop == 1 and unit[0] == TAIL
+        low = kept(unit, hop)
         if way == -1:
-            return jnp.logical_and(z > (1 if later else 0), z + hop - 1 <= n - 1)
-        return jnp.logical_and(z < n - (2 if later else 1), z - (hop - 1) >= 0)
+            return jnp.logical_and(z > low, z + hop - 1 <= n - 1)
+        return jnp.logical_and(z < n - 1 - low, z - (hop - 1) >= 0)
 
     def gets(unit, way, hop):
-        later = hop == 1 and unit[0] == TAIL
+        low = kept(unit, hop)
         if way == -1:
-            return jnp.logical_and(z >= (1 if later else 0), z + hop <= n - 1)
-        return jnp.logical_and(z <= n - (2 if later else 1), z - hop >= 0)
+            return jnp.logical_and(z >= low, z + hop <= n - 1)
+        return jnp.logical_and(z <= n - 1 - low, z - hop >= 0)
 
     def start_ring(unit):
         for way in (-1, 1):
@@ -226,9 +234,11 @@
 
     def send_own(c):
         start_ring((c, 0))
+        keep(c).start()
+
+    def send_plane(c):
         for k in order:
             plane(c, k).start()
-        keep(c).start()
 
     def add_up(first, size):
         @pl.loop(0, size // LANES)
@@ -236,20 +246,27 @@
             parts = quantize_rows(stage, pl.ds(pl.multiple_of(first + t * LANES, LANES), LANES), spread, floor)
             next(parts)
             for b, part in enumerate(parts):
-                acc[b] += jnp.sum(part.astype(jnp.float32).reshape(LANES // 8, 8, LANES), axis=0)
-
-    arrange(0)
+                both = part.astype(jnp.float32)
+                for i in range(2):
+                    one = both[:, i * LANES:(i + 1) * LANES].reshape(LANES // 8, 8, LANES)
+                    acc[2 * b + i] += jnp.sum(one, axis=0)
+
+    arrange(HEAD)
     pl.semaphore_wait(barrier, count - 1 + beside)
-    send_own(0)
-    arrange(1)
-    for c in range(2, chunks):
-        arrange(c)
-        send_own(c - 1)
+    send_own(HEAD)
+    arrange(BODY)
+    send_own(BODY)
+    arrange(ODD)
+    send_plane(MAIN)
+    arrange(TAIL)
+    send_own(ODD)
+    send_plane(ODD)
     acc[...] = jnp.zeros_like(acc)
     write_spread(spread, nblocks)
-    add_up(*spans[0])
+    add_up(*spans[HEAD])
     send_own(TAIL)
-    add_up(spans[0][1], rows - spans[0][1])
+    send_plane(TAIL)
+    add_up(spans[HEAD][1], rows - spans[HEAD][1])
 
     sums = jnp.sum(jnp.sum(acc[...], axis=1), axis=1, keepdims=True)
     row = lax.broadcasted_iota(jnp.int32, (nblocks, LANES), 0)
@@ -257,18 +274,19 @@
     line = jnp.sum(jnp.where(row == col, sums, 0.0), axis=0, keepdims=True)
     zsum[z] = jnp.broadcast_to(line, zsum.shape[1:])
 
-    blocks = [(c, k) for c in range(chunks) for k in [0] + order]
+    blocks = [(HEAD, 0), (BODY, 0)] + [(MAIN, k) for k in order] + [(c, k) for c in (ODD, TAIL) for k in [0] + order]
     for c, k in blocks:
         if k > 0:
             plane(c, k).wait_recv()
             start_ring((c, k))
-            if (c, k) == (0, order[-1]):
+            if (c, k) == (MAIN, order[0]):
                 start_ring((SUM, 0))
 
+    keep(ODD).wait()
     keep(TAIL).wait()
-    start = spans[TAIL][0]
+    start = spans[ODD][0]
     tail_out = []
-    for i, ref in enumerate((tail_ref, last_ref)):
+    for i, ref in enumerate((odd_ref, tail_ref, last_ref)):
         here = pl.ds(pl.multiple_of(z * rows + start + i * LANES, 16), LANES)
         tail_out.append(pltpu.make_async_copy(out_ref.at[here], ref, tail_sem.at[i]))
     for copy in tail_out:
@@ -298,9 +316,9 @@
     psum[m] = whole
     for copy in tail_out:
         copy.wait()
-    for c in range(chunks):
-        if c != TAIL:
-            keep(c).wait()
+    for c in (HEAD, BODY):
+        keep(c).wait()
+    for c in (MAIN, ODD, TAIL):
         for k in order:
             plane(c, k).wait_send()
     for k in order:
@@ -330,9 +348,10 @@
     return pl.pallas_call(
         functools.partial(move_kernel, n, count, spans, floor),
         in_specs=[pl.BlockSpec(memory_space=pltpu.SMEM), any_spec],
-        out_specs=[any_spec] + [pl.BlockSpec(memory_space=pltpu.VMEM)] * 3,
+        out_specs=[any_spec] + [pl.BlockSpec(memory_space=pltpu.VMEM)] * 4,
         out_shape=[
             jax.ShapeDtypeStruct((n * rows, cols), weight.dtype),
+            jax.ShapeDtypeStruct((LANES, cols), weight.dtype),
             jax.ShapeDtypeStruct((LANES, cols), weight.dtype),
             jax.ShapeDtypeStruct((LANES, cols), weight.dtype),
             jax.ShapeDtypeStruct((count, 8, LANES), jnp.float32),
@@ -347,7 +366,7 @@
             pltpu.VMEM((count, 8, LANES), jnp.float32),
             dma((chunks,)),
             dma((chunks,)),
-            dma((2,)),
+            dma((3,)),
             dma((chunks + 1, count - 1)),
             dma((chunks + 1, count - 1)),
             dma((2, n - 1, chunks + 1, count)),
@@ -361,19 +380,22 @@
 def local(n, weight, rank_map):
     rows, cols = weight.shape
     nblocks = cols // LANES
+    count = rank_map.shape[0]
     total_rows = rows * n
     floor = FLOOR_RATIO / math.sqrt(total_rows)
-    main = rows - 2 * LANES
-    rest = (main - LANES) // 2
-    spans = ((0, LANES), (LANES, rest), (LANES + rest, rest), (main, 2 * LANES))
+    main = rows - 3 * LANES
+    spans = ((0, main), (main, LANES), (main + LANES, 2 * LANES), (0, LANES), (LANES, main - LANES))
     ends = [(1, 0), (n - 2, n - 1)]
-
-    landed, tail_own, last_own, sums = move(weight, rank_map, n, spans, floor)
+    even = [(a * count + m, b * count + m) for a, b in ends for m in range(0, count, 2)]
+
+    landed, odd_own, tail_own, last_own, sums = move(weight, rank_map, n, spans, floor)
+    odd_got = lax.ppermute(odd_own, ("dp", "mp"), even)
     tail_got = lax.ppermute(tail_own, "dp", ends)
     last_got = lax.ppermute(last_own, "dp", ends)
     quant, scale = quantize_all(landed, floor)
-    quant, scale = fill(quant, scale, tail_got, n, rows, main, floor)
-    quant, scale = fill(quant, scale, last_got, n, rows, main + LANES, floor)
+    quant, scale = fill(quant, scale, odd_got, n, rows, main, True, floor)
+    quant, scale = fill(quant, scale, tail_got, n, rows, main + LANES, False, floor)
+    quant, scale = fill(quant, scale, last_got, n, rows, main + 2 * LANES, False, floor)
     totals = sums[:, 0, :nblocks].reshape(-1)
     return (quant, scale.T, totals / (127.0 * math.sqrt(total_rows * LANES)))
 

time: 702 us -> 689 us (0.981)
  Pallas kernels: 696 us -> 667 us
  waiting for transfers between devices: 0.01 us -> 15.1 us
    pallas_call x1, Pallas kernels: 644 us -> 624 us  [move(): pl.pallas_call(functools.partial(move_kernel, n, count, spans, floor), in...]
    ppermute x1, waiting for transfers between devices: 0.01 us -> 15.1 us  [local(): last_got = lax.ppermute(last_own, 'dp', ends)]
    pallas_call x1, Pallas kernels: 47.4 us -> 37.2 us  [quantize_all(): pl.pallas_call(functools.partial(quantize_kernel, floor), grid=(rows // t...]
  transfers between devices with their start and end apart: 2 -> 3, of which waited for: 0 -> 1; matrix products, arithmetic and copies ran while one was open for 0% -> 0% of each run, Pallas kernels for 7% -> 6%
where the time goes in v2:
time: 689 us; the launch traced here: 688 us
  Pallas kernels  667 us (97%)
  waiting for transfers between devices  15.1 us (2%)
    pallas_call x1, Pallas kernels, move(): pl.pallas_call(functools.partial(move_kernel, n, count, spans, floor), in...  624 us
    pallas_call x1, Pallas kernels, quantize_all(): pl.pallas_call(functools.partial(quantize_kernel, floor), grid=(rows // t...  37.2 us
    ppermute x1, waiting for transfers between devices, local(): last_got = lax.ppermute(last_own, 'dp', ends)  15.1 us
  transfers between devices with their start and end apart: 3, of which 1 were waited for; matrix products, arithmetic and copies ran while one was open for 0% of the time, Pallas kernels for 6%

profile of v2, /device:TPU:0, one launch (start us, length us, event | category | flops | bytes accessed | tf_op | source)
XLA Modules:
  0.0 688.4 jit_solution(7962865389607167900)
XLA Ops:
  0.6 623.8 %shard_map.49 = (bf16[5120,4096]{1,0:T(8,128)(2,1)}, bf16[128,4096]{1,0:T(8,128)(2,1)}, bf16[128,4096]{1,0:T(8,128)(2,1)}, bf16[128,4096]{1,0:T(8,128)(2,1)}, f32[8,8,128]{2,1,0:T(8,128)}) custom-call(s32[8]{0:T(128)} %map_ref.1, bf16[1280,4096]{1,0:T(8,128)(2,1)} %w_ref.1), custom_call_target="tpu_custom_call" | custom-call | flops 41943040 | bytes 62914560 | tf_op jit(solution)/shard_map/pallas_call | solution.py:348
  624.5 1.3 collective-permute-start.2
  625.8 1.3 collective-permute-start.1
  627.1 1.3 collective-permute-start
  628.4 0.8 multiply_reduce_fusion
  629.2 0.6 div.10
  629.8 37.2 %shard_map.50 = (bf16[5120,4096]{1,0:T(8,128)(2,1)}, bf16[32,5120]{1,0:T(8,128)(2,1)}) custom-call(bf16[5120,4096]{1,0:T(8,128)(2,1)} %get-tuple-element.19.x_ref), custom_call_target="tpu_custom_call" | custom-call | flops 83886080 | bytes 83886080 | tf_op jit(solution)/shard_map/pallas_call | solution.py:84
  667.0 0.0 collective-permute-done.2.got_ref
  667.0 2.1 shard_map.51
  669.1 0.0 collective-permute-done.1.got_ref
  669.1 2.1 shard_map.52
  671.2 15.1 %collective-permute-done.got_ref = bf16[128,4096]{1,0:T(8,128)(2,1)S(1)} collective-permute-done((bf16[128,4096]{1,0:T(8,128)(2,1)}, bf16[128,4096]{1,0:T(8,128)(2,1)S(1)}, u32[]{:S(2)}, u32[]{:S(2)}) %collective-permute-start) | collective-permute-done | bytes 1048608 | tf_op jit(solution)/shard_map/ppermute | solution.py:394
  686.3 2.1 shard_map.53
Async XLA Ops:
  624.5 42.5 %collective-permute-start.2 = (bf16[128,4096]{1,0:T(8,128)(2,1)}, bf16[128,4096]{1,0:T(8,128)(2,1)S(1)}, u32[]{:S(2)}, u32[]{:S(2)}) collective-permute-start(bf16[128,4096]{1,0:T(8,128)(2,1)} %get-tuple-element.18), channel_id=1, source_target_pairs={{8,0},{10,2},{12,4},{14,6},{16,24},{18,26},{20,28},{22,30}} | collective-permute-start | bytes 3145736 | tf_op jit(solution)/shard_map/ppermute | solution.py:392
  625.8 43.3 %collective-permute-start.1 = (bf16[128,4096]{1,0:T(8,128)(2,1)}, bf16[128,4096]{1,0:T(8,128)(2,1)S(1)}, u32[]{:S(2)}, u32[]{:S(2)}) collective-permute-start(bf16[128,4096]{1,0:T(8,128)(2,1)} %get-tuple-element.17), channel_id=1, source_target_pairs={{8,0},{16,24},{9,1},{17,25},{10,2},{18,26},{11,3},{19,27},{12,4},{... | collective-permute-start | bytes 3145736 | tf_op jit(solution)/shard_map/ppermute | solution.py:393
  627.1 59.2 %collective-permute-start = (bf16[128,4096]{1,0:T(8,128)(2,1)}, bf16[128,4096]{1,0:T(8,128)(2,1)S(1)}, u32[]{:S(2)}, u32[]{:S(2)}) collective-permute-start(bf16[128,4096]{1,0:T(8,128)(2,1)} %get-tuple-element.16), channel_id=1, source_target_pairs={{8,0},{16,24},{9,1},{17,25},{10,2},{18,26},{11,3},{19,27},{12,4},{... | collective-permute-start | bytes 3145736 | tf_op jit(solution)/shard_map/ppermute | solution.py:394

commit v3 on v2

--- a/solution.py
+++ b/solution.py
@@ -135,7 +135,7 @@
 
 def move_kernel(n, count, spans, floor, map_ref, w_ref, out_ref, odd_ref, tail_ref, last_ref, sum_ref,
                 stage, perm, spread, acc, zsum, total, psum,
-                load_sem, own_sem, tail_sem, a_send, a_recv, z_send, z_recv):
+                load_sem, own_sem, tail_sem, a_send, a_recv, z_send, z_recv, p_send, p_recv, s_send, s_recv):
     z = lax.axis_index("dp")
     m = lax.axis_index("mp")
     rows, width = perm.shape[1:]
@@ -179,6 +179,9 @@
                         block = jnp.where(holds[r][j], blocks[j], block)
                     perm[r, here, i * LANES:(i + 1) * LANES] = block
 
+    blocks = [(HEAD, 0), (BODY, 0)] + [(MAIN, k) for k in order] + [(c, k) for c in (ODD, TAIL) for k in [0] + order]
+    slots = {unit: slot for slot, unit in enumerate(blocks)}
+
     def place(origin, c, src):
         start, size = spans[c]
         return out_ref.at[pl.ds(pl.multiple_of(origin * rows + start, 16), size),
@@ -190,25 +193,30 @@
     def plane(c, k):
         peer = flip(m, k)
         if c == SUM:
-            src, dst = total, psum.at[m]
+            src, dst, send, recv = total, psum.at[m], p_send.at[k - 1], p_recv.at[k - 1]
         else:
             src, dst = perm.at[peer, pl.ds(*spans[c])], place(z, c, m)
+            send, recv = a_send.at[c], a_recv.at[c, k - 1]
         return pltpu.make_async_remote_copy(
-            src_ref=src, dst_ref=dst, send_sem=a_send.at[c, k - 1], recv_sem=a_recv.at[c, k - 1],
-            device_id=(z, peer), device_id_type=MESH)
-
-    def ring(unit, way, hop):
+            src_ref=src, dst_ref=dst, send_sem=send, recv_sem=recv, device_id=(z, peer), device_id_type=MESH)
+
+    def ring(unit, way, hop, got=False):
         c, k = unit
-        origin = z - way * (hop - 1)
+        origin = z + way * -hop if got else z - way * (hop - 1)
+        w = 0 if way == 1 else 1
         if c == SUM:
             src = dst = zsum.at[origin]
+            send, recv = s_send.at[w, hop - 1], s_recv.at[origin]
         else:
             dst = place(origin, c, flip(m, k))
-            src = own(c) if hop == 1 and k == 0 else dst
-        w = 0 if way == 1 else 1
+            src = own(c) if hop == 1 and k == 0 and not got else dst
+            send, recv = z_send.at[w, hop - 1, min(c, HEAD) % HEAD], z_recv.at[origin, slots[unit]]
         return pltpu.make_async_remote_copy(
-            src_ref=src, dst_ref=dst, send_sem=z_send.at[w, hop - 1, c, k], recv_sem=z_recv.at[w, hop - 1, c, k],
+            src_ref=src, dst_ref=dst, send_sem=send, recv_sem=recv,
             device_id=(z + way, m), device_id_type=MESH)
+
+    def sent(refs, sem):
+        pltpu.make_async_copy(refs, refs, sem).wait()
 
     def kept(unit, hop):
         return {TAIL: 1, ODD: 1 - m % 2}.get(unit[0], 0) if hop == 1 else 0
@@ -274,7 +282,6 @@
     line = jnp.sum(jnp.where(row == col, sums, 0.0), axis=0, keepdims=True)
     zsum[z] = jnp.broadcast_to(line, zsum.shape[1:])
 
-    blocks = [(HEAD, 0), (BODY, 0)] + [(MAIN, k) for k in order] + [(c, k) for c in (ODD, TAIL) for k in [0] + order]
     for c, k in blocks:
         if k > 0:
             plane(c, k).wait_recv()
@@ -285,10 +292,13 @@
     keep(ODD).wait()
     keep(TAIL).wait()
     start = spans[ODD][0]
-    tail_out = []
-    for i, ref in enumerate((odd_ref, tail_ref, last_ref)):
-        here = pl.ds(pl.multiple_of(z * rows + start + i * LANES, 16), LANES)
-        tail_out.append(pltpu.make_async_copy(out_ref.at[here], ref, tail_sem.at[i]))
+    size = rows - start
+    tail = pl.ds(pl.multiple_of(z * rows + start, 16), size)
+    tail_in = pltpu.make_async_copy(out_ref.at[tail], stage.at[pl.ds(0, size)], tail_sem.at[0])
+    tail_in.start()
+    tail_in.wait()
+    tail_out = [pltpu.make_async_copy(stage.at[pl.ds(i * LANES, LANES)], ref, tail_sem.at[i + 1])
+                for i, ref in enumerate((odd_ref, tail_ref, last_ref))]
     for copy in tail_out:
         copy.start()
 
@@ -297,14 +307,14 @@
         for unit in units:
             for way in (-1, 1):
                 def forward(unit=unit, way=way, hop=hop):
-                    ring(unit, way, hop - 1).wait_recv()
+                    ring(unit, way, hop - 1, True).wait_recv()
                     ring(unit, way, hop).start()
 
                 when(sends(unit, way, hop), forward)
 
     def settle(unit, way, hop):
         stays = z == 0 if way == -1 else z == n - 1
-        when(jnp.logical_and(gets(unit, way, hop), stays), lambda: ring(unit, way, hop).wait_recv())
+        when(jnp.logical_and(gets(unit, way, hop), stays), lambda: ring(unit, way, hop, True).wait_recv())
 
     for hop in range(1, n):
         for way in (-1, 1):
@@ -319,21 +329,27 @@
     for c in (HEAD, BODY):
         keep(c).wait()
     for c in (MAIN, ODD, TAIL):
-        for k in order:
-            plane(c, k).wait_send()
+        sent(perm.at[pl.ds(0, count - 1), pl.ds(*spans[c])], a_send.at[c])
     for k in order:
         plane(SUM, k).start()
     for k in order:
         plane(SUM, k).wait()
-    sum_ref[...] = psum[...]
-
+    sums_out = pltpu.make_async_copy(psum, sum_ref, tail_sem.at[0])
+    sums_out.start()
     for hop in range(1, n):
-        for unit in units:
+        for way in (-1, 1):
+            when(sends((SUM, 0), way, hop), lambda way=way, hop=hop: ring((SUM, 0), way, hop).wait_send())
+    sums_out.wait()
+
+    for hop in range(1, n):
+        for unit in blocks:
             for way in (-1, 1):
-                if unit[0] != SUM:
-                    settle(unit, way, hop)
-                when(sends(unit, way, hop),
-                     lambda unit=unit, way=way, hop=hop: ring(unit, way, hop).wait_send())
+                settle(unit, way, hop)
+        for c in (MAIN, ODD, TAIL):
+            for way in (-1, 1):
+                w = 0 if way == 1 else 1
+                when(sends((c, 0), way, hop),
+                     lambda c=c, w=w, hop=hop: sent(out_ref.at[pl.ds(*spans[c])], z_send.at[w, hop - 1, c]))
 
 
 def move(weight, rank_map, n, spans, floor):
@@ -348,7 +364,7 @@
     return pl.pallas_call(
         functools.partial(move_kernel, n, count, spans, floor),
         in_specs=[pl.BlockSpec(memory_space=pltpu.SMEM), any_spec],
-        out_specs=[any_spec] + [pl.BlockSpec(memory_space=pltpu.VMEM)] * 4,
+        out_specs=[any_spec] + [any_spec] * 4,
         out_shape=[
             jax.ShapeDtypeStruct((n * rows, cols), weight.dtype),
             jax.ShapeDtypeStruct((LANES, cols), weight.dtype),
@@ -366,11 +382,15 @@
             pltpu.VMEM((count, 8, LANES), jnp.float32),
             dma((chunks,)),
             dma((chunks,)),
+            dma((4,)),
             dma((3,)),
-            dma((chunks + 1, count - 1)),
-            dma((chunks + 1, count - 1)),
-            dma((2, n - 1, chunks + 1, count)),
-            dma((2, n - 1, chunks + 1, count)),
+            dma((3, count - 1)),
+            dma((2, n - 1, 3)),
+            dma((n, 3 * count + 1)),
+            dma((count - 1,)),
+            dma((count - 1,)),
+            dma((2, n - 1)),
+            dma((n,)),
         ],
         compiler_params=pltpu.CompilerParams(collective_id=0, has_side_effects=True, vmem_limit_bytes=VMEM_LIMIT),
         cost_estimate=pl.CostEstimate(flops=rows * cols * 8, bytes_accessed=sent * 2, transcendentals=0),

time: 689 us -> 686 us (level)
  no operation moved by 1% of the time
where the time goes in v3:
time: 686 us; the launch traced here: 685 us
  Pallas kernels  661 us (96%)
  waiting for transfers between devices  18.1 us (3%)
    pallas_call x1, Pallas kernels, move(): pl.pallas_call(functools.partial(move_kernel, n, count, spans, floor), in...  618 us
    pallas_call x1, Pallas kernels, quantize_all(): pl.pallas_call(functools.partial(quantize_kernel, floor), grid=(rows // t...  37.1 us
    ppermute x1, waiting for transfers between devices, local(): last_got = lax.ppermute(last_own, 'dp', ends)  18.1 us
  transfers between devices with their start and end apart: 3, of which 1 were waited for; matrix products, arithmetic and copies ran while one was open for 0% of the time, Pallas kernels for 6%

profile of v3, /device:TPU:0, one launch (start us, length us, event | category | flops | bytes accessed | tf_op | source)
XLA Modules:
  0.0 685.4 jit_solution(1213833004408224571)
XLA Ops:
  0.6 617.8 %shard_map.49 = (bf16[5120,4096]{1,0:T(8,128)(2,1)}, bf16[128,4096]{1,0:T(8,128)(2,1)}, bf16[128,4096]{1,0:T(8,128)(2,1)}, bf16[128,4096]{1,0:T(8,128)(2,1)}, f32[8,8,128]{2,1,0:T(8,128)}) custom-call(s32[8]{0:T(128)} %map_ref.1, bf16[1280,4096]{1,0:T(8,128)(2,1)} %w_ref.1), custom_call_target="tpu_custom_call" | custom-call | flops 41943040 | bytes 62914560 | tf_op jit(solution)/shard_map/pallas_call | solution.py:364
  618.4 1.3 collective-permute-start.2
  619.7 1.3 collective-permute-start.1
  621.0 1.3 collective-permute-start
  622.3 0.8 multiply_reduce_fusion
  623.1 0.6 div.10
  623.8 37.1 %shard_map.50 = (bf16[5120,4096]{1,0:T(8,128)(2,1)}, bf16[32,5120]{1,0:T(8,128)(2,1)}) custom-call(bf16[5120,4096]{1,0:T(8,128)(2,1)} %get-tuple-element.19.x_ref), custom_call_target="tpu_custom_call" | custom-call | flops 83886080 | bytes 83886080 | tf_op jit(solution)/shard_map/pallas_call | solution.py:84
  660.9 0.0 collective-permute-done.2.got_ref
  660.9 2.1 shard_map.51
  663.0 0.0 collective-permute-done.1.got_ref
  663.0 2.1 shard_map.52
  665.1 18.1 %collective-permute-done.got_ref = bf16[128,4096]{1,0:T(8,128)(2,1)S(1)} collective-permute-done((bf16[128,4096]{1,0:T(8,128)(2,1)}, bf16[128,4096]{1,0:T(8,128)(2,1)S(1)}, u32[]{:S(2)}, u32[]{:S(2)}) %collective-permute-start) | collective-permute-done | bytes 1048608 | tf_op jit(solution)/shard_map/ppermute | solution.py:414
  683.3 2.1 shard_map.53
Async XLA Ops:
  618.4 42.4 %collective-permute-start.2 = (bf16[128,4096]{1,0:T(8,128)(2,1)}, bf16[128,4096]{1,0:T(8,128)(2,1)S(1)}, u32[]{:S(2)}, u32[]{:S(2)}) collective-permute-start(bf16[128,4096]{1,0:T(8,128)(2,1)} %get-tuple-element.18), channel_id=1, source_target_pairs={{8,0},{10,2},{12,4},{14,6},{16,24},{18,26},{20,28},{22,30}} | collective-permute-start | bytes 3145736 | tf_op jit(solution)/shard_map/ppermute | solution.py:412
  619.7 43.3 %collective-permute-start.1 = (bf16[128,4096]{1,0:T(8,128)(2,1)}, bf16[128,4096]{1,0:T(8,128)(2,1)S(1)}, u32[]{:S(2)}, u32[]{:S(2)}) collective-permute-start(bf16[128,4096]{1,0:T(8,128)(2,1)} %get-tuple-element.17), channel_id=1, source_target_pairs={{8,0},{16,24},{9,1},{17,25},{10,2},{18,26},{11,3},{19,27},{12,4},{... | collective-permute-start | bytes 3145736 | tf_op jit(solution)/shard_map/ppermute | solution.py:413
  621.0 62.2 %collective-permute-start = (bf16[128,4096]{1,0:T(8,128)(2,1)}, bf16[128,4096]{1,0:T(8,128)(2,1)S(1)}, u32[]{:S(2)}, u32[]{:S(2)}) collective-permute-start(bf16[128,4096]{1,0:T(8,128)(2,1)} %get-tuple-element.16), channel_id=1, source_target_pairs={{8,0},{16,24},{9,1},{17,25},{10,2},{18,26},{11,3},{19,27},{12,4},{... | collective-permute-start | bytes 3145736 | tf_op jit(solution)/shard_map/ppermute | solution.py:414

commit v4 on v3

--- a/solution.py
+++ b/solution.py
@@ -103,12 +103,18 @@
     @pl.when(end)
     def _():
         write_spread(spread, s_v.shape[0])
-        quantize_tile(floor, got_ref, q_v, s_v, spread)
-        place = pl.ds(pl.multiple_of(jnp.where(z == 0, 1, n - 2) * rows + first, LANES), q_v.shape[0])
-        copies = [pltpu.make_async_copy(q_v, q_ref.at[place], sems.at[0]),
-                  pltpu.make_async_copy(s_v, s_ref.at[:, place], sems.at[1])]
-        for copy in copies:
-            copy.start()
+        size, half = q_v.shape[1:]
+        place = pl.ds(pl.multiple_of(jnp.where(z == 0, 1, n - 2) * rows + first, LANES), size)
+        parts = quantize_rows(got_ref, pl.ds(0, size), spread, floor)
+        s_v[...] = next(parts).T[:s_v.shape[0]].astype(jnp.bfloat16)
+        copies = [pltpu.make_async_copy(s_v, s_ref.at[:, place], sems.at[2])]
+        copies[0].start()
+        wide = 2 * LANES
+        for side in range(2):
+            for col in range(0, half, wide):
+                q_v[side, :, col:col + wide] = next(parts)
+            copies.append(pltpu.make_async_copy(q_v.at[side], q_ref.at[place, pl.ds(side * half, half)], sems.at[side]))
+            copies[-1].start()
         for copy in copies:
             copy.wait()
 
@@ -123,10 +129,10 @@
         out_shape=[jax.ShapeDtypeStruct(quant.shape, quant.dtype), jax.ShapeDtypeStruct(scale.shape, scale.dtype)],
         input_output_aliases={1: 0, 2: 1},
         scratch_shapes=[
-            pltpu.VMEM((size, cols), quant.dtype),
+            pltpu.VMEM((2, size, cols // 2), quant.dtype),
             pltpu.VMEM((scale.shape[0], size), scale.dtype),
             pltpu.VMEM((LANES, cols), jnp.bfloat16),
-            pltpu.SemaphoreType.DMA((2,)),
+            pltpu.SemaphoreType.DMA((3,)),
         ],
         compiler_params=pltpu.CompilerParams(vmem_limit_bytes=FILL_LIMIT),
         cost_estimate=pl.CostEstimate(flops=size * cols * 4, bytes_accessed=size * cols * 4, transcendentals=0),

time: 686 us -> 686 us (level)
  no operation moved by 1% of the time
where the time goes in v4:
time: 686 us; the launch traced here: 685 us
  Pallas kernels  661 us (96%)
  waiting for transfers between devices  18.4 us (3%)
    pallas_call x1, Pallas kernels, move(): pl.pallas_call(functools.partial(move_kernel, n, count, spans, floor), in...  618 us
    pallas_call x1, Pallas kernels, quantize_all(): pl.pallas_call(functools.partial(quantize_kernel, floor), grid=(rows // t...  37.1 us
    ppermute x1, waiting for transfers between devices, local(): last_got = lax.ppermute(last_own, 'dp', ends)  18.4 us
  transfers between devices with their start and end apart: 3, of which 1 were waited for; matrix products, arithmetic and copies ran while one was open for 0% of the time, Pallas kernels for 6%

profile of v4, /device:TPU:0, one launch (start us, length us, event | category | flops | bytes accessed | tf_op | source)
XLA Modules:
  0.0 685.3 jit_solution(1925576015817569472)
XLA Ops:
  0.6 617.8 %shard_map.49 = (bf16[5120,4096]{1,0:T(8,128)(2,1)}, bf16[128,4096]{1,0:T(8,128)(2,1)}, bf16[128,4096]{1,0:T(8,128)(2,1)}, bf16[128,4096]{1,0:T(8,128)(2,1)}, f32[8,8,128]{2,1,0:T(8,128)}) custom-call(s32[8]{0:T(128)} %map_ref.1, bf16[1280,4096]{1,0:T(8,128)(2,1)} %w_ref.1), custom_call_target="tpu_custom_call" | custom-call | flops 41943040 | bytes 62914560 | tf_op jit(solution)/shard_map/pallas_call | solution.py:370
  618.4 1.3 collective-permute-start.2
  619.7 1.3 collective-permute-start.1
  621.0 1.3 collective-permute-start
  622.3 0.8 multiply_reduce_fusion
  623.1 0.6 div.10
  623.8 37.1 %shard_map.50 = (bf16[5120,4096]{1,0:T(8,128)(2,1)}, bf16[32,5120]{1,0:T(8,128)(2,1)}) custom-call(bf16[5120,4096]{1,0:T(8,128)(2,1)} %get-tuple-element.19.x_ref), custom_call_target="tpu_custom_call" | custom-call | flops 83886080 | bytes 83886080 | tf_op jit(solution)/shard_map/pallas_call | solution.py:84
  660.9 0.0 collective-permute-done.2.got_ref
  660.9 2.0 shard_map.51
  662.9 0.0 collective-permute-done.1.got_ref
  662.9 2.0 shard_map.52
  664.9 18.4 %collective-permute-done.got_ref = bf16[128,4096]{1,0:T(8,128)(2,1)S(1)} collective-permute-done((bf16[128,4096]{1,0:T(8,128)(2,1)}, bf16[128,4096]{1,0:T(8,128)(2,1)S(1)}, u32[]{:S(2)}, u32[]{:S(2)}) %collective-permute-start) | collective-permute-done | bytes 1048608 | tf_op jit(solution)/shard_map/ppermute | solution.py:420
  683.3 2.0 shard_map.53
Async XLA Ops:
  618.4 42.4 %collective-permute-start.2 = (bf16[128,4096]{1,0:T(8,128)(2,1)}, bf16[128,4096]{1,0:T(8,128)(2,1)S(1)}, u32[]{:S(2)}, u32[]{:S(2)}) collective-permute-start(bf16[128,4096]{1,0:T(8,128)(2,1)} %get-tuple-element.18), channel_id=1, source_target_pairs={{8,0},{10,2},{12,4},{14,6},{16,24},{18,26},{20,28},{22,30}} | collective-permute-start | bytes 3145736 | tf_op jit(solution)/shard_map/ppermute | solution.py:418
  619.7 43.1 %collective-permute-start.1 = (bf16[128,4096]{1,0:T(8,128)(2,1)}, bf16[128,4096]{1,0:T(8,128)(2,1)S(1)}, u32[]{:S(2)}, u32[]{:S(2)}) collective-permute-start(bf16[128,4096]{1,0:T(8,128)(2,1)} %get-tuple-element.17), channel_id=1, source_target_pairs={{8,0},{16,24},{9,1},{17,25},{10,2},{18,26},{11,3},{19,27},{12,4},{... | collective-permute-start | bytes 3145736 | tf_op jit(solution)/shard_map/ppermute | solution.py:419
  621.0 62.2 %collective-permute-start = (bf16[128,4096]{1,0:T(8,128)(2,1)}, bf16[128,4096]{1,0:T(8,128)(2,1)S(1)}, u32[]{:S(2)}, u32[]{:S(2)}) collective-permute-start(bf16[128,4096]{1,0:T(8,128)(2,1)} %get-tuple-element.16), channel_id=1, source_target_pairs={{8,0},{16,24},{9,1},{17,25},{10,2},{18,26},{11,3},{19,27},{12,4},{... | collective-permute-start | bytes 3145736 | tf_op jit(solution)/shard_map/ppermute | solution.py:420
